TPU v7x, 32 devices: a whole 2x2x4 slice. The times are simulated.
32 devices in a mesh: dp: 2 (over x), tp: 16 (over y, z, core).
Axes of the slice: x: 2, y: 2, z: 4, core: 2. Of those that a mesh axis runs over, the one named last changes fastest.
Arguments:
- x: bfloat16 [128, 4096], P('dp'), parts along dimension 0
- k_cache: bfloat16 [128, 2048, 64, 64], P('dp', None, 'tp'), parts along dimension 0
- v_cache: bfloat16 [128, 2048, 64, 64], P('dp', None, 'tp'), parts along dimension 0
- gain_a: bfloat16 [4096], replicated
- wq: bfloat16 [4096, 4096], P(None, 'tp')
- wo: bfloat16 [4096, 4096], P('tp')
- gain_m: bfloat16 [4096], replicated
- w_gate: bfloat16 [4096, 10240], P(None, 'tp')
- w_up: bfloat16 [4096, 10240], P(None, 'tp')
- w_down: bfloat16 [10240, 4096], P('tp')
Outputs:
- output: bfloat16 [128, 4096], P('dp'), parts along dimension 0
There are 2 independent parts. A program takes and returns all parts, laid end to end along the dimension named above; an argument that names none is the same for every part.
All inputs are finite; a program needn't handle non-finite values.
Results may differ from a plain program's by a relative error of at most 0.017.
Values are sent between devices in bfloat16 or wider.
A program may use at most 2 GiB of HBM per device.

v0:
```python
import jax
import jax.numpy as jnp
from jax import lax
from jax.sharding import PartitionSpec as P

HEAD = 64
THETA = 10000


def normed(x, gain):
    wide = x.astype(jnp.float32)
    scale = lax.rsqrt(jnp.mean(wide * wide, -1, keepdims=True) + 1e-6)
    return (wide * scale * gain.astype(jnp.float32)).astype(jnp.bfloat16)


def turned(t, place, theta):
    half = t.shape[-1] // 2
    angle = place.astype(jnp.float32)[:, None] * theta ** (-jnp.arange(half, dtype=jnp.float32) / half)
    cos, sin = jnp.cos(angle)[:, None], jnp.sin(angle)[:, None]
    a, b = t[..., :half].astype(jnp.float32), t[..., half:].astype(jnp.float32)
    return jnp.concatenate([a * cos - b * sin, b * cos + a * sin], -1).astype(jnp.bfloat16)


def matmul(a, w):
    return jnp.dot(a, w, preferred_element_type=jnp.float32).astype(jnp.bfloat16)


def einsum(form, a, b):
    return jnp.einsum(form, a.astype(jnp.float32), b.astype(jnp.float32))


def seen_by(a, wq, k_cache, v_cache, head, theta):
    batch, cache, kv_heads = k_cache.shape[:3]
    place = jnp.full((batch,), cache - 1)
    q = turned(matmul(a, wq).reshape(batch, -1, head), place, theta).reshape(batch, kv_heads, -1, head)
    scores = einsum("bgsd,bugd->bgsu", q, k_cache) * head**-0.5
    weights = jax.nn.softmax(scores, -1).astype(jnp.bfloat16)
    return einsum("bgsu,bugd->bgsd", weights, v_cache).astype(jnp.bfloat16).reshape(batch, -1)


def hidden_of(b, w_gate, w_up):
    gate = jnp.dot(b, w_gate, preferred_element_type=jnp.float32)
    up = jnp.dot(b, w_up, preferred_element_type=jnp.float32)
    return (jax.nn.silu(gate) * up).astype(jnp.bfloat16)


def solution(mesh):
    def added(t, term):
        return (t.astype(jnp.float32) + lax.psum(term.astype(jnp.bfloat16), "tp").astype(jnp.float32)).astype(jnp.bfloat16)

    def step(x, k_cache, v_cache, gain_a, wq, wo, gain_m, w_gate, w_up, w_down):
        seen = seen_by(normed(x, gain_a), wq, k_cache, v_cache, HEAD, THETA)
        h = added(x, jnp.dot(seen, wo, preferred_element_type=jnp.float32))
        return added(h, jnp.dot(hidden_of(normed(h, gain_m), w_gate, w_up), w_down, preferred_element_type=jnp.float32))

    states, cache, columns, rows_of = P("dp", None), P("dp", None, "tp", None), P(None, "tp"), P("tp", None)
    return jax.shard_map(
        step,
        mesh=mesh,
        in_specs=(states, cache, cache, P(None), columns, rows_of, P(None), columns, columns, rows_of),
        out_specs=states,
        check_vma=False,
    )
```

profile of v0, /device:TPU:0, one launch (start us, length us, event | category | flops | bytes accessed | tf_op | source)
XLA Modules:
  0.0 273.3 jit_solution(8626443076888678604)
XLA Ops:
  6.5 0.0 copy-start
  6.5 0.0 all-reduce.3.cloned.1.call-start
  6.6 0.8 convert_element_type.66
  7.4 1.2 fusion.11
  8.7 2.3 convolution_convert_fusion.2
  11.0 0.1 copy.11
  11.1 0.1 fusion.34
  11.2 0.1 copy.12
  11.4 24.0 %fusion.45 = f32[64,4,1,2048]{3,2,1,0:T(1,128)} fusion(bf16[64,4,64,1]{2,3,1,0:T(2,128)(2,1)S(1)} %copy.12, bf16[64,2048,4,64]{1,3,2,0:T(8,128)(2,1)} %param.11), kind=kOutput, calls=%fused_computation.58 | convolution fusion | flops 67108864 | bytes 69238784 | tf_op jit(solution)/shard_map/bgsd,bugd->bgsu/dot_general | solution.py:29
  35.4 4.3 %fusion.6 = bf16[64,4,2048,1]{2,0,1,3:T(8,128)(2,1)S(1)} fusion(f32[64,4,1,2048]{3,2,1,0:T(1,128)} %fusion.45), kind=kOutput, calls=%fused_computation.8 | output fusion | flops 2101758 | bytes 3145728 | tf_op jit(solution)/shard_map/div | solution.py:37
  39.7 25.7 %fusion.7 = f32[64,4,1,64]{3,2,1,0:T(1,128)S(1)} fusion(bf16[64,2048,4,64]{1,3,2,0:T(8,128)(2,1)} %param.12, bf16[64,4,2048,1]{2,0,1,3:T(8,128)(2,1)S(1)} %fusion.6), kind=kOutput, calls=%fused_computation.10 | convolution fusion | flops 67108864 | bytes 68222976 | tf_op jit(solution)/shard_map/bgsu,bugd->bgsd/dot_general | solution.py:29
  65.4 0.0 copy-start.2
  65.4 0.0 copy-start.1
  65.4 0.1 reshape.62
  65.6 1.3 convolution_convert_fusion.1
  66.8 0.0 all-reduce.3.cloned.1.call-update
  66.9 0.0 all-reduce.5.cloned.1.call-start
  66.9 94.7 %all-reduce.3.cloned.1.call-done = bf16[64,4096]{1,0:T(8,128)(2,1)} async-done(((bf16[64,4096]{1,0:T(8,128)(2,1)}), bf16[64,4096]{1,0:T(8,128)(2,1)}) %all-reduce.3.cloned.1.call-update) | async-done | bytes 524304 | tf_op jit(solution)/shard_map/psum | solution.py:49
  161.6 1.3 fusion.15
  163.0 3.6 %fusion.30 = f32[64,640]{1,0:T(8,128)S(1)} fusion(bf16[4096,640]{1,0:T(8,128)(2,1)} %param.17, bf16[64,4096]{1,0:T(8,128)(2,1)S(1)} %get-tuple-element.6, f32[4096]{0:T(1024)S(1)} %convert_element_type.77, f32[64]{0:T(128)S(1)} %add_rsqrt_fusion), kind=kOutput, calls=%fused_computation.38 | convolution fusion | flops 336592896 | bytes 5947648 | tf_op jit(solution)/shard_map/dot_general | solution.py:42
  166.5 6.9 %convolution_convert_fusion = bf16[64,4096]{1,0:T(8,128)(2,1)} fusion(bf16[640,4096]{1,0:T(8,128)(2,1)} %param.19, bf16[4096,640]{1,0:T(8,128)(2,1)} %param.18, f32[64,640]{1,0:T(8,128)S(1)} %fusion.30, bf16[64,4096]{1,0:T(8,128)(2,1)S(1)} %get-tuple-element.6, f32[4096]{0:T(1024)S(1)} %convert_element_type.77, f32[64]{0:T(128)S(1)} %add_rsqrt_fusion), kind=kOutput, calls=%fused_computation.2 | convolution fusion | flops 672645120 | bytes 11714816 | tf_op jit(solution)/shard_map/dot_general | solution.py:54
  173.4 0.0 all-reduce.5.cloned.1.call-update
  173.4 91.1 %all-reduce.5.cloned.1.call-done = bf16[64,4096]{1,0:T(8,128)(2,1)} async-done(((bf16[64,4096]{1,0:T(8,128)(2,1)}), bf16[64,4096]{1,0:T(8,128)(2,1)}) %all-reduce.5.cloned.1.call-update) | async-done | bytes 524304 | tf_op jit(solution)/shard_map/psum | solution.py:49
  264.5 2.0 fusion.18
  (9 shorter events, 0.1 us)
Async XLA Ops:
  6.5 59.0 %copy-start = (bf16[256,4096]{1,0:T(8,128)(2,1)S(1)}, bf16[256,4096]{1,0:T(8,128)(2,1)}, u32[]{:S(2)}) copy-start(bf16[256,4096]{1,0:T(8,128)(2,1)} %param.15) | copy-start | bytes 6291460
  6.5 155.1 %all-reduce.3.cloned.1.call-start = ((), (), s32[]{:S(2)}) async-start(), calls=%async_computation | async-start | bytes 1048576 | tf_op jit(solution)/shard_map/psum | solution.py:49
  65.4 1.5 copy-start.2
  65.4 96.2 %copy-start.1 = (bf16[64,4096]{1,0:T(8,128)(2,1)S(1)}, bf16[64,4096]{1,0:T(8,128)(2,1)}, u32[]{:S(2)}) copy-start(bf16[64,4096]{1,0:T(8,128)(2,1)} %param.10) | copy-start | bytes 1572868
  66.9 197.6 %all-reduce.5.cloned.1.call-start = ((), (), s32[]{:S(2)}) async-start(), calls=%async_computation.1 | async-start | bytes 1048576 | tf_op jit(solution)/shard_map/psum | solution.py:49
Sparse Core Ops, SparseCore 0:
  67.0 94.5 all-reduce.2
  173.5 90.8 all-reduce.4
where the time goes:
time: 274 us; the launch traced here: 273 us
  waiting for transfers between devices  186 us (68%)
  matrix products  63.7 us (23%)
  between operations  13.5 us (5%)
  other arithmetic  9.86 us (4%)
    psum x2, waiting for transfers between devices, added(): lax.psum(term.astype(jnp.bfloat16), 'tp').astype(jnp.float32)  186 us
    dot_general x2, matrix products, einsum(): return jnp.einsum(form, a.astype(jnp.float32), b.astype(jnp.float32))  49.7 us
    dot_general x1, matrix products, step(): jnp.dot(hidden_of(normed(h, gain_m), w_gate, w_up), w_down, preferred_ele...  6.87 us
  transfers between devices with their start and end apart: 2, of which 2 were waited for; matrix products, arithmetic and copies ran while one was open for 0% of the time, Pallas kernels for 0%

commit v1 on v0

v1 whole, which is shorter than its diff:
```python
import functools

import jax
import jax.numpy as jnp
import numpy as np
from jax import lax
from jax.experimental import pallas as pl
from jax.experimental.pallas import tpu as pltpu
from jax.sharding import PartitionSpec as P

HEAD = 64
THETA = 10000
BF16, F32 = jnp.bfloat16, jnp.float32

N = 16
D = 4096
W = D // N
HL = 4
QW = HL * HEAD
FL = 640
B = 64
U = 2048
G = 4
NC = B // G
NS = 4
R = 16
NG = B // R
CPG = R // G
LAG = 3
TICKS = NC + 4 * LAG


def tables():
    half = HEAD // 2
    angle = np.float32(U - 1) * np.float32(THETA) ** (-np.arange(half, dtype=np.float32) / np.float32(half))
    cos, sin = np.cos(angle.astype(np.float64)), np.sin(angle.astype(np.float64))
    cos = np.tile(np.concatenate([cos, cos]), HL)
    sin = np.tile(np.concatenate([-sin, sin]), HL)
    return np.stack([np.broadcast_to(cos, (8, QW)), np.broadcast_to(sin, (8, QW))]).astype(np.float32)


def kernel(
    x_hbm, k_hbm, v_hbm, ga_hbm, wq_hbm, wo_hbm, gm_hbm, wg_hbm, wu_hbm, wd_hbm, cs_hbm, out_hbm,
    xs, ab, qbd, wq, wo, wgu, wd, ga, gm, cs, kbuf, vbuf, wts, seen, bs,
    send1, recv1, hs, send2, recv2, ys,
    misc_sem, ksem, vsem, wsem, osem, s1, r1, s2, r2, s3, r3, s4, r4,
):
    me = lax.axis_index("tp")
    barrier = pltpu.get_barrier_semaphore()
    for k in range(1, N):
        pl.semaphore_signal(barrier, inc=1, device_id={"tp": lax.rem(me + k, N)}, device_id_type=pl.DeviceIdType.MESH)

    def local(src, dst, sem):
        return pltpu.make_async_copy(src, dst, sem)

    def kcopy(c):
        rows = pl.ds(pl.multiple_of(c * (G * QW), G * QW), G * QW)
        return local(k_hbm.at[rows], kbuf.at[lax.rem(c, NS)], ksem.at[lax.rem(c, NS)])

    def vcopy(c):
        rows = pl.ds(pl.multiple_of(c * (G * QW), G * QW), G * QW)
        return local(v_hbm.at[rows], vbuf.at[lax.rem(c, NS)], vsem.at[lax.rem(c, NS)])

    first = [
        local(x_hbm, xs, misc_sem.at[0]),
        local(ga_hbm, ga, misc_sem.at[1]),
        local(wq_hbm, wq, misc_sem.at[2]),
        local(cs_hbm, cs, misc_sem.at[3]),
        local(gm_hbm, gm, misc_sem.at[4]),
    ]
    for c in first:
        c.start()
    for c in range(NS):
        kcopy(jnp.int32(c)).start()
        vcopy(jnp.int32(c)).start()
    wo_copy = local(wo_hbm, wo, wsem.at[0])
    wg_copy = local(wg_hbm, wgu.at[:, pl.ds(0, FL)], wsem.at[1])
    wu_copy = local(wu_hbm, wgu.at[:, pl.ds(FL, FL)], wsem.at[2])
    wd_copy = local(wd_hbm, wd, wsem.at[3])

    first[0].wait()
    first[1].wait()
    gain = ga[...].astype(F32)
    for r in range(0, B, R):
        wide = xs[r:r + R, :].astype(F32)
        scale = lax.rsqrt(jnp.mean(wide * wide, -1, keepdims=True) + 1e-6)
        for j in range(D // 128):
            cols = slice(128 * j, 128 * j + 128)
            ab[r:r + R, cols] = (wide[:, cols] * scale * gain[j:j + 1, :]).astype(BF16)
    first[2].wait()
    q = jnp.dot(ab[...], wq[...], preferred_element_type=F32).astype(BF16).astype(F32)
    first[3].wait()
    first[4].wait()
    lane = lax.broadcasted_iota(jnp.int32, (B, QW), 1)
    rot = jnp.where(lax.rem(lane, HEAD) < HEAD // 2, pltpu.roll(q, QW - HEAD // 2, 1), pltpu.roll(q, HEAD // 2, 1))
    cosines, sines = cs[0, 0:1, :], cs[1, 0:1, :]
    q = (q * cosines + rot * sines).astype(BF16).astype(F32)
    row = lax.broadcasted_iota(jnp.int32, (G * HL, QW), 0)
    col = lax.broadcasted_iota(jnp.int32, (G * HL, QW), 1)
    for c in range(NC):
        for i in range(G):
            line = jnp.broadcast_to(q[c * G + i:c * G + i + 1, :], (G * HL, QW))
            line = jnp.where(col // HEAD + HL * i == row, line, 0.0)
            qbd[c, :, QW * i:QW * (i + 1)] = line.astype(BF16)

    def scores(c):
        kcopy(c).wait()
        return jnp.dot(qbd[c], kbuf[lax.rem(c, NS)], preferred_element_type=F32)

    def softmax(s, c):
        top = jnp.max(s, -1, keepdims=True)
        p = jnp.exp((s - top) * HEAD**-0.5)
        wts[lax.rem(c, 2)] = (p / jnp.sum(p, -1, keepdims=True)).astype(BF16)

    def values(c):
        vcopy(c).wait()
        return lax.dot_general(wts[lax.rem(c, 2)], vbuf[lax.rem(c, NS)], (((1,), (1,)), ((), ())), preferred_element_type=F32)

    def keep(o, c):
        grp = c // CPG
        base = lax.rem(c, CPG) * G
        total = seen[grp]
        for i in range(G):
            part = o[:, QW * i:QW * (i + 1)]
            part = jnp.where(col // HEAD + HL * i == row, part, 0.0)
            line = jnp.broadcast_to(jnp.sum(part, 0, keepdims=True), (R, QW))
            total = jnp.where(row == base + i, line, total)
        seen[grp] = total

    def scatter(send, recv, ssem, rsem, g):
        for k in range(1, N):
            to = lax.rem(me + k, N)
            pltpu.make_async_remote_copy(
                src_ref=send.at[g, to], dst_ref=recv.at[g, k - 1], send_sem=ssem.at[g], recv_sem=rsem.at[g],
                device_id={"tp": to}, device_id_type=pl.DeviceIdType.MESH,
            ).start()

    def gather(buf, ssem, rsem, g):
        for k in range(1, N):
            to = lax.rem(me + k, N)
            pltpu.make_async_remote_copy(
                src_ref=buf.at[g, me], dst_ref=buf.at[g, me], send_sem=ssem.at[g], recv_sem=rsem.at[g],
                device_id={"tp": to}, device_id_type=pl.DeviceIdType.MESH,
            ).start()

    def arrived(buf, ssem, rsem, g):
        whole = buf.at[g, pl.ds(0, N - 1)]
        done = pltpu.make_async_remote_copy(
            src_ref=whole, dst_ref=whole, send_sem=ssem.at[g], recv_sem=rsem.at[g],
            device_id={"tp": lax.rem(me + 1, N)}, device_id_type=pl.DeviceIdType.MESH,
        )
        done.wait_send()
        done.wait_recv()

    def summed(send, recv, g):
        total = send[g, me].astype(F32)
        for k in range(N - 1):
            total = total + recv[g, k].astype(F32)
        return total

    def stage1(g):
        o = jnp.dot(seen[g].astype(BF16), wo[...], preferred_element_type=F32)
        for j in range(N):
            send1[g, j] = o[:, W * j:W * (j + 1)].astype(BF16)
        scatter(send1, recv1, s1, r1, g)

    def stage2(g):
        arrived(recv1, s1, r1, g)
        rows = pl.ds(pl.multiple_of(g * R, R), R)
        cols = pl.ds(pl.multiple_of(me * W, W), W)
        hs[g, me] = (xs[rows, cols].astype(F32) + summed(send1, recv1, g)).astype(BF16)
        gather(hs, s2, r2, g)

    def stage3(g):
        arrived(hs, s2, r2, g)
        square = jnp.zeros((R, W), F32)
        for j in range(N):
            wide = hs[g, j].astype(F32)
            square = square + wide * wide
        scale = lax.rsqrt(jnp.sum(square, -1, keepdims=True) * (1.0 / D) + 1e-6)
        gain = gm[...].astype(F32)
        for j in range(N):
            wide = hs[g, j].astype(F32) * scale
            for i in range(2):
                n = 2 * j + i
                bs[:, 128 * n:128 * n + 128] = (wide[:, 128 * i:128 * i + 128] * gain[n:n + 1, :]).astype(BF16)
        both = jnp.dot(bs[...], wgu[...], preferred_element_type=F32)
        gate, up = both[:, :FL], both[:, FL:]
        hidden = (gate * jax.nn.sigmoid(gate) * up).astype(BF16)
        o = jnp.dot(hidden, wd[...], preferred_element_type=F32)
        for j in range(N):
            send2[g, j] = o[:, W * j:W * (j + 1)].astype(BF16)
        scatter(send2, recv2, s3, r3, g)

    def stage4(g):
        arrived(recv2, s3, r3, g)
        ys[g, me] = (hs[g, me].astype(F32) + summed(send2, recv2, g)).astype(BF16)
        gather(ys, s4, r4, g)

    def stage5(g):
        arrived(ys, s4, r4, g)
        local(ys.at[g], out_hbm.at[g], osem.at[g]).start()

    softmax(scores(jnp.int32(0)), jnp.int32(0))
    kcopy(jnp.int32(NS)).start()

    def tick(t, carry):
        @pl.when(t < NC - 1)
        def _():
            s = scores(t + 1)
            o = values(t)
            softmax(s, t + 1)
            keep(o, t)

        @pl.when(t == NC - 1)
        def _():
            keep(values(t), t)

        @pl.when(t + 1 + NS < NC)
        def _():
            kcopy(t + 1 + NS).start()

        @pl.when(t + NS < NC)
        def _():
            vcopy(t + NS).start()

        for at, copy in ((0, wo_copy), (2, wg_copy), (4, wu_copy), (6, wd_copy)):
            pl.when(t == at)(copy.start)

        @pl.when(t == CPG - 1)
        def _():
            wo_copy.wait()
            pl.semaphore_wait(barrier, N - 1)

        @pl.when(t == CPG - 1 + 2 * LAG)
        def _():
            wg_copy.wait()
            wu_copy.wait()
            wd_copy.wait()

        for i, stage in enumerate((stage1, stage2, stage3, stage4, stage5)):
            since = t - (CPG - 1) - LAG * i
            due = (since >= 0) & (lax.rem(since, CPG) == 0) & (since < CPG * NG)
            pl.when(due)(functools.partial(stage, since // CPG))
        return carry

    lax.fori_loop(0, TICKS, tick, 0)
    for g in range(NG):
        local(ys.at[g], out_hbm.at[g], osem.at[g]).wait()


def layer(x, k_cache, v_cache, gain_a, wq, wo, gain_m, w_gate, w_up, w_down):
    k = jnp.transpose(k_cache, (0, 2, 3, 1)).reshape(B * QW, U)
    v = jnp.transpose(v_cache, (0, 2, 3, 1)).reshape(B * QW, U)
    dma, vmem = pltpu.SemaphoreType.DMA, pltpu.VMEM
    out = pl.pallas_call(
        kernel,
        out_shape=jax.ShapeDtypeStruct((NG, N, R, W), BF16),
        in_specs=[pl.BlockSpec(memory_space=pl.ANY)] * 11,
        out_specs=pl.BlockSpec(memory_space=pl.ANY),
        scratch_shapes=[
            vmem((B, D), BF16), vmem((B, D), BF16), vmem((NC, G * HL, G * QW), BF16),
            vmem((D, QW), BF16), vmem((QW, D), BF16), vmem((D, 2 * FL), BF16), vmem((FL, D), BF16),
            vmem((D // 128, 128), BF16), vmem((D // 128, 128), BF16), vmem((2, 8, QW), F32),
            vmem((NS, G * QW, U), BF16), vmem((NS, G * QW, U), BF16), vmem((2, G * HL, U), BF16),
            vmem((NG, R, QW), F32), vmem((R, D), BF16),
            vmem((NG, N, R, W), BF16), vmem((NG, N - 1, R, W), BF16), vmem((NG, N, R, W), BF16),
            vmem((NG, N, R, W), BF16), vmem((NG, N - 1, R, W), BF16), vmem((NG, N, R, W), BF16),
            dma((5,)), dma((NS,)), dma((NS,)), dma((4,)), dma((NG,)),
        ] + [dma((NG,))] * 8,
        compiler_params=pltpu.CompilerParams(collective_id=0, has_side_effects=True, vmem_limit_bytes=67043328),
        name="layer",
    )(x, k, v, gain_a.reshape(D // 128, 128), wq, wo, gain_m.reshape(D // 128, 128), w_gate, w_up, w_down, jnp.asarray(tables()))
    return out.transpose(0, 2, 1, 3).reshape(B, D)


def solution(mesh):
    states, cache, columns, rows_of = P("dp", None), P("dp", None, "tp", None), P(None, "tp"), P("tp", None)
    return jax.shard_map(
        layer,
        mesh=mesh,
        in_specs=(states, cache, cache, P(None), columns, rows_of, P(None), columns, columns, rows_of),
        out_specs=states,
        check_vma=False,
    )
```

time: 274 us -> 89.1 us (0.33)
  waiting for transfers between devices: 186 us -> 0 us
  Pallas kernels: 0 us -> 86.8 us
  matrix products: 63.7 us -> 0 us
  between operations: 13.5 us -> 0.01 us
  other arithmetic: 9.86 us -> 0 us
    psum x2 -> x0, waiting for transfers between devices: 186 us -> none  [added(): lax.psum(term.astype(jnp.bfloat16), 'tp').astype(jnp.float32)]
    pallas_call x0 -> x1, Pallas kernels: none -> 86.8 us  [layer(): pl.pallas_call(kernel, out_shape=jax.ShapeDtypeStruct((NG, N, R, W), BF16...]
    dot_general x6 -> x0, matrix products: 63.7 us -> none  [the longest x2 49.7 us: einsum(): return jnp.einsum(form, a.astype(jnp.float32), b.astype(jnp.float32))]
    div x1 -> x0, other arithmetic: 4.29 us -> none  [seen_by(): weights = jax.nn.softmax(scores, -1).astype(jnp.bfloat16)]
    convert_element_type x4 -> x0, other arithmetic: 2.83 us -> none  [the longest x1 1.96 us: added(): (t.astype(jnp.float32) + lax.psum(term.astype(jnp.bfloat16), 'tp').astype...]
  transfers between devices with their start and end apart: 2 -> 0, of which waited for: 2 -> 0; matrix products, arithmetic and copies ran while one was open for 0% -> 0% of each run, Pallas kernels for 0% -> 0%
where the time goes in v1:
time: 89.1 us; the launch traced here: 89 us
  Pallas kernels  86.8 us (97%)
  local copies, waits for them, and re-layouts  2.18 us (2%)
    pallas_call x1, Pallas kernels, layer(): pl.pallas_call(kernel, out_shape=jax.ShapeDtypeStruct((NG, N, R, W), BF16...  86.8 us

profile of v1, /device:TPU:0, one launch (start us, length us, event | category | flops | bytes accessed | tf_op | source)
XLA Modules:
  0.0 89.0 jit_solution(17906628530615723023)
XLA Ops:
  0.0 86.8 %layer.1 = bf16[4,16,16,256]{3,2,1,0:T(8,128)(2,1)} custom-call(bf16[64,4096]{1,0:T(8,128)(2,1)} %x_hbm.1, bf16[16384,2048]{1,0:T(8,128)(2,1)} %bitcast.1.k_hbm, bf16[16384,2048]{1,0:T(8,128)(2,1)} %bitcast.3.v_hbm, bf16[32,128]{1,0:T(8,128)(2,1)} %bitcast.14, bf16[4096,256]{1,0:T(8,128)(2,1)} %wq_hbm.1, bf16[256,4096]{1,0:T(8,128)(2,1)} %wo_hbm.1, ...), custom_call_target="tpu_custom_call" | custom-call | tf_op jit(solution)/shard_map/layer/pallas_call | solution.py:256
  86.8 1.2 %copy.12 = bf16[4,16,16,256]{3,2,1,0:T(8,128)(2,1)S(1)} copy(bf16[4,16,16,256]{3,1,2,0:T(8,128)(2,1)} %bitcast.12) | data formatting | bytes 1048576 | tf_op jit(solution)/shard_map/transpose | solution.py:274
  88.0 1.0 %copy.13 = bf16[8,8,16,256]{3,1,2,0:T(8,128)(2,1)} copy(bf16[8,8,16,256]{3,2,1,0:T(8,128)(2,1)S(1)} %bitcast.13) | data formatting | bytes 1048576

commit v2 on v1

v2 whole, which is shorter than its diff:
```python
import functools

import jax
import jax.numpy as jnp
import numpy as np
from jax import lax
from jax.experimental import pallas as pl
from jax.experimental.pallas import tpu as pltpu
from jax.sharding import PartitionSpec as P

HEAD = 64
THETA = 10000
BF16, F32 = jnp.bfloat16, jnp.float32

N = 16
D = 4096
W = D // N
HL = 4
QW = HL * HEAD
FL = 640
B = 64
U = 2048
G = 4
NC = B // G
NS = 4
ROWS = (16, 16, 16, 8, 8)
NG = len(ROWS)
FIRST = tuple(sum(ROWS[:g]) for g in range(NG))
Q, Z = 4, 4
DURING = {
    3: ((1, 0),), 5: ((2, 0),), 7: ((1, 1), (3, 0)), 9: ((2, 1), (4, 0)), 11: ((1, 2), (3, 1), (5, 0)),
    13: ((1, 3), (2, 2)), 14: ((6, 0),), 15: ((1, 4), (3, 2), (2, 3)),
}
AFTER = (
    (4, 1), (2, 4), (7, 0), (3, 3), (4, 2), (5, 1), (3, 4), (4, 3), (5, 2), (4, 4), (6, 1), (5, 3), (6, 2), (5, 4),
    (7, 1), (6, 3), (7, 2), (6, 4), (7, 3), (7, 4),
)
LM = G * HL


def tables():
    half = HEAD // 2
    angle = np.float32(U - 1) * np.float32(THETA) ** (-np.arange(half, dtype=np.float32) / np.float32(half))
    cos, sin = np.cos(angle.astype(np.float64)), np.sin(angle.astype(np.float64))
    cos = np.tile(np.concatenate([cos, cos]), HL)
    sin = np.tile(np.concatenate([-sin, sin]), HL)
    return np.stack([np.broadcast_to(cos, (8, QW)), np.broadcast_to(sin, (8, QW))]).astype(np.float32)


def kernel(
    x_hbm, k_hbm, v_hbm, ga_hbm, wq_hbm, wo_hbm, gm_hbm, wg_hbm, wu_hbm, wd_hbm, cs_hbm, out,
    xs, ab, qbd, wq, wo, wgu, wd, ga, gm, cs, kbuf, vbuf, wts, seen, bs,
    misc_sem, ksem, vsem, wsem, ssem, rsem, *parts,
):
    terms1, near1, line1, hs, terms2, near2, line2, ys = (parts[NG * i:NG * (i + 1)] for i in range(8))
    me = lax.axis_index("tp")
    barrier = pltpu.get_barrier_semaphore()
    for k in range(1, N):
        pl.semaphore_signal(barrier, inc=1, device_id={"tp": lax.rem(me + k, N)}, device_id_type=pl.DeviceIdType.MESH)

    def local(src, dst, sem):
        return pltpu.make_async_copy(src, dst, sem)

    def kcopy(c):
        rows = pl.ds(pl.multiple_of(c * (G * QW), G * QW), G * QW)
        return local(k_hbm.at[rows], kbuf.at[lax.rem(c, NS)], ksem.at[lax.rem(c, NS)])

    def vcopy(c):
        rows = pl.ds(pl.multiple_of(c * (G * QW), G * QW), G * QW)
        return local(v_hbm.at[rows], vbuf.at[lax.rem(c, NS)], vsem.at[lax.rem(c, NS)])

    first = [
        local(x_hbm, xs, misc_sem.at[0]),
        local(ga_hbm, ga, misc_sem.at[1]),
        local(wq_hbm, wq, misc_sem.at[2]),
        local(cs_hbm, cs, misc_sem.at[3]),
        local(gm_hbm, gm, misc_sem.at[4]),
    ]
    for c in first:
        c.start()
    kcopy(jnp.int32(0)).start()
    wo_copy = local(wo_hbm, wo, wsem.at[0])
    wg_copy = local(wg_hbm, wgu.at[:, pl.ds(0, FL)], wsem.at[1])
    wu_copy = local(wu_hbm, wgu.at[:, pl.ds(FL, FL)], wsem.at[2])
    wd_copy = local(wd_hbm, wd, wsem.at[3])

    first[0].wait()
    first[1].wait()
    gain = ga[...].astype(F32)
    for r in range(0, B, 16):
        wide = xs[r:r + 16, :].astype(F32)
        scale = lax.rsqrt(jnp.mean(wide * wide, -1, keepdims=True) + 1e-6)
        for j in range(D // 128):
            cols = slice(128 * j, 128 * j + 128)
            ab[r:r + 16, cols] = (wide[:, cols] * scale * gain[j:j + 1, :]).astype(BF16)
    first[2].wait()
    vcopy(jnp.int32(0)).start()
    kcopy(jnp.int32(1)).start()
    vcopy(jnp.int32(1)).start()
    q = jnp.dot(ab[...], wq[...], preferred_element_type=F32).astype(BF16).astype(F32)
    first[3].wait()
    first[4].wait()
    lane = lax.broadcasted_iota(jnp.int32, (B, QW), 1)
    rot = jnp.where(lax.rem(lane, HEAD) < HEAD // 2, pltpu.roll(q, QW - HEAD // 2, 1), pltpu.roll(q, HEAD // 2, 1))
    cosines, sines = cs[0, 0:1, :], cs[1, 0:1, :]
    q = (q * cosines + rot * sines).astype(BF16).astype(F32)
    row = lax.broadcasted_iota(jnp.int32, (LM, QW), 0)
    col = lax.broadcasted_iota(jnp.int32, (LM, QW), 1)
    for c in range(NC):
        for i in range(G):
            line = jnp.broadcast_to(q[c * G + i:c * G + i + 1, :], (LM, QW))
            line = jnp.where(col // HEAD + HL * i == row, line, 0.0)
            qbd[c, :, QW * i:QW * (i + 1)] = line.astype(BF16)

    def scores(c):
        kcopy(c).wait()
        return jnp.dot(qbd[c], kbuf[lax.rem(c, NS)], preferred_element_type=F32)

    def softmax(s, c):
        top = jnp.max(s, -1, keepdims=True)
        p = jnp.exp((s - top) * HEAD**-0.5)
        wts[lax.rem(c, 2)] = (p / jnp.sum(p, -1, keepdims=True)).astype(BF16)

    def values(c):
        vcopy(c).wait()
        return lax.dot_general(wts[lax.rem(c, 2)], vbuf[lax.rem(c, NS)], (((1,), (1,)), ((), ())), preferred_element_type=F32)

    def keep(o, c):
        block = lax.div(c * G, 8)
        base = lax.rem(c * G, 8)
        total = seen[block]
        sub = lax.broadcasted_iota(jnp.int32, (8, QW), 0)
        for i in range(G):
            part = o[:, QW * i:QW * (i + 1)]
            part = jnp.where(col // HEAD + HL * i == row, part, 0.0)
            line = jnp.broadcast_to(jnp.sum(part, 0, keepdims=True), (8, QW))
            total = jnp.where(sub == base + i, line, total)
        seen[block] = total

    y, z, core = me // 8, lax.rem(me // 2, Z), lax.rem(me, 2)
    mine = y * 2 + core

    def send(src, dst, phase, g, to):
        pltpu.make_async_remote_copy(
            src_ref=src, dst_ref=dst, send_sem=ssem.at[phase, g], recv_sem=rsem.at[phase, g],
            device_id={"tp": to}, device_id_type=pl.DeviceIdType.MESH,
        ).start()

    def arrived(whole, phase, g):
        done = pltpu.make_async_remote_copy(
            src_ref=whole, dst_ref=whole, send_sem=ssem.at[phase, g], recv_sem=rsem.at[phase, g],
            device_id={"tp": lax.rem(me + 1, N)}, device_id_type=pl.DeviceIdType.MESH,
        )
        done.wait_send()
        done.wait_recv()

    def in_plane(k):
        other = lax.rem(mine + k, Q)
        return other, (other // 2) * 8 + z * 2 + lax.rem(other, 2)

    def scatter(terms, near, phase, g):
        for k in range(1, Q):
            other, to = in_plane(k)
            send(terms[g].at[pl.ds(other * Q, Q)], near[g].at[k - 1], phase, g, to)

    def along(terms, near, line, phase, g):
        arrived(near[g], phase, g)
        for j in range(Q):
            total = terms[g][mine * Q + j].astype(F32)
            for k in range(Q - 1):
                total = total + near[g][k, j].astype(F32)
            line[g][z, j] = total.astype(BF16)
        for k in range(1, Z):
            send(line[g].at[z], line[g].at[z], phase + 1, g, y * 8 + lax.rem(z + k, Z) * 2 + core)

    def gather(line, buf, residual, phase, g):
        arrived(line[g].at[pl.ds(0, Z - 1)], phase + 1, g)
        for j in range(Q):
            total = line[g][0, j].astype(F32)
            for k in range(1, Z):
                total = total + line[g][k, j].astype(F32)
            buf[g][mine * Q + j] = (residual(j) + total).astype(BF16)
        for k in range(1, Q):
            _, to = in_plane(k)
            own = buf[g].at[pl.ds(mine * Q, Q)]
            send(own, own, phase + 2, g, to)

    def gathered(buf, phase, g):
        arrived(buf[g].at[pl.ds(0, N - Q)], phase + 2, g)

    def stage1(g):
        rows = seen[FIRST[g] // 8:(FIRST[g] + ROWS[g]) // 8].reshape(ROWS[g], QW)
        o = jnp.dot(rows.astype(BF16), wo[...], preferred_element_type=F32)
        for j in range(N):
            terms1[g][j] = o[:, W * j:W * (j + 1)].astype(BF16)
        scatter(terms1, near1, 0, g)

    def stage2(g):
        along(terms1, near1, line1, 0, g)

    def stage3(g):
        def residual(j):
            cols = pl.ds(pl.multiple_of((mine * Q + j) * W, W), W)
            return xs[FIRST[g]:FIRST[g] + ROWS[g], cols].astype(F32)

        gather(line1, hs, residual, 0, g)

    def stage4(g):
        gathered(hs, 0, g)
        square = jnp.zeros((ROWS[g], W), F32)
        for j in range(N):
            wide = hs[g][j].astype(F32)
            square = square + wide * wide
        scale = lax.rsqrt(jnp.sum(square, -1, keepdims=True) * (1.0 / D) + 1e-6)
        gain = gm[...].astype(F32)
        for j in range(N):
            wide = hs[g][j].astype(F32) * scale
            for i in range(2):
                n = 2 * j + i
                bs[:ROWS[g], 128 * n:128 * n + 128] = (wide[:, 128 * i:128 * i + 128] * gain[n:n + 1, :]).astype(BF16)
        both = jnp.dot(bs[:ROWS[g], :], wgu[...], preferred_element_type=F32)
        gate, up = both[:, :FL], both[:, FL:]
        hidden = (gate * jax.nn.sigmoid(gate) * up).astype(BF16)
        o = jnp.dot(hidden, wd[...], preferred_element_type=F32)
        for j in range(N):
            terms2[g][j] = o[:, W * j:W * (j + 1)].astype(BF16)
        scatter(terms2, near2, 3, g)

    def stage5(g):
        along(terms2, near2, line2, 3, g)

    def stage6(g):
        gather(line2, ys, lambda j: hs[g][mine * Q + j].astype(F32), 3, g)

    def stage7(g):
        gathered(ys, 3, g)
        for j in range(N):
            out[FIRST[g]:FIRST[g] + ROWS[g], W * j:W * (j + 1)] = ys[g][j]

    kcopy(jnp.int32(2)).start()
    vcopy(jnp.int32(2)).start()
    softmax(scores(jnp.int32(0)), jnp.int32(0))
    kcopy(jnp.int32(3)).start()
    vcopy(jnp.int32(3)).start()
    kcopy(jnp.int32(NS)).start()

    def tick(t, carry):
        @pl.when(t < NC - 1)
        def _():
            s = scores(t + 1)
            o = values(t)
            softmax(s, t + 1)
            keep(o, t)

        @pl.when(t == NC - 1)
        def _():
            keep(values(t), t)

        @pl.when(t + 1 + NS < NC)
        def _():
            kcopy(t + 1 + NS).start()

        @pl.when(t + NS < NC)
        def _():
            vcopy(t + NS).start()

        for at, copy in ((0, wo_copy), (2, wg_copy), (4, wu_copy), (6, wd_copy)):
            pl.when(t == at)(copy.start)

        for at, due in DURING.items():
            @pl.when(t == at)
            def _(due=due):
                if (1, 0) in due:
                    wo_copy.wait()
                    pl.semaphore_wait(barrier, N - 1)
                if (4, 0) in due:
                    wg_copy.wait()
                    wu_copy.wait()
                    wd_copy.wait()
                for n, g in due:
                    stages[n - 1](g)
        return carry

    stages = (stage1, stage2, stage3, stage4, stage5, stage6, stage7)
    lax.fori_loop(0, NC, tick, 0)
    for n, g in AFTER:
        stages[n - 1](g)


def layer(x, k_cache, v_cache, gain_a, wq, wo, gain_m, w_gate, w_up, w_down):
    k = jnp.transpose(k_cache, (0, 2, 3, 1)).reshape(B * QW, U)
    v = jnp.transpose(v_cache, (0, 2, 3, 1)).reshape(B * QW, U)
    dma, vmem = pltpu.SemaphoreType.DMA, pltpu.VMEM
    return pl.pallas_call(
        kernel,
        out_shape=pltpu.VMEM((B, D), BF16),
        in_specs=[pl.BlockSpec(memory_space=pl.ANY)] * 11,
        out_specs=pl.BlockSpec(memory_space=pltpu.VMEM),
        scratch_shapes=[
            vmem((B, D), BF16), vmem((B, D), BF16), vmem((NC, LM, G * QW), BF16),
            vmem((D, QW), BF16), vmem((QW, D), BF16), vmem((D, 2 * FL), BF16), vmem((FL, D), BF16),
            vmem((D // 128, 128), BF16), vmem((D // 128, 128), BF16), vmem((2, 8, QW), F32),
            vmem((NS, G * QW, U), BF16), vmem((NS, G * QW, U), BF16), vmem((2, LM, U), BF16),
            vmem((B // 8, 8, QW), F32), vmem((max(ROWS), D), BF16),
            dma((5,)), dma((NS,)), dma((NS,)), dma((4,)),
            dma((6, NG)), dma((6, NG)),
        ] + [vmem((*n, r, W), BF16) for n in ((N,), (Q - 1, Q), (Z, Q), (N,)) * 2 for r in ROWS],
        compiler_params=pltpu.CompilerParams(collective_id=0, has_side_effects=True, vmem_limit_bytes=65994752),
        name="layer",
    )(x, k, v, gain_a.reshape(D // 128, 128), wq, wo, gain_m.reshape(D // 128, 128), w_gate, w_up, w_down, jnp.asarray(tables()))


def solution(mesh):
    states, cache, columns, rows_of = P("dp", None), P("dp", None, "tp", None), P(None, "tp"), P("tp", None)
    return jax.shard_map(
        layer,
        mesh=mesh,
        in_specs=(states, cache, cache, P(None), columns, rows_of, P(None), columns, columns, rows_of),
        out_specs=states,
        check_vma=False,
    )
```

time: 89.1 us -> 78 us (0.88)
  Pallas kernels: 86.8 us -> 77 us
  local copies, waits for them, and re-layouts: 2.18 us -> 0.8 us
    pallas_call x1, Pallas kernels: 86.8 us -> 77 us  [layer(): pl.pallas_call(kernel, out_shape=pltpu.VMEM((B, D), BF16), in_specs=[pl.B...]
    transpose x1 -> x0, local copies, waits for them, and re-layouts: 1.21 us -> none  [layer(): return out.transpose(0, 2, 1, 3).reshape(B, D)]
where the time goes in v2:
time: 78 us; the launch traced here: 77.8 us
  Pallas kernels  77 us (99%)
  local copies, waits for them, and re-layouts  0.8 us (1%)
    pallas_call x1, Pallas kernels, layer(): pl.pallas_call(kernel, out_shape=pltpu.VMEM((B, D), BF16), in_specs=[pl.B...  77 us

profile of v2, /device:TPU:0, one launch (start us, length us, event | category | flops | bytes accessed | tf_op | source)
XLA Modules:
  0.0 77.8 jit_solution(17651260783122718501)
XLA Ops:
  0.0 77.0 %layer.1 = bf16[64,4096]{1,0:T(8,128)(2,1)S(1)} custom-call(bf16[64,4096]{1,0:T(8,128)(2,1)} %x_hbm.1, bf16[16384,2048]{1,0:T(8,128)(2,1)} %bitcast.1.k_hbm, bf16[16384,2048]{1,0:T(8,128)(2,1)} %bitcast.3.v_hbm, bf16[32,128]{1,0:T(8,128)(2,1)} %bitcast.8, bf16[4096,256]{1,0:T(8,128)(2,1)} %wq_hbm.1, bf16[256,4096]{1,0:T(8,128)(2,1)} %wo_hbm.1, ...), custom_call_target="tpu_custom_call" | custom-call | tf_op jit(solution)/shard_map/layer/pallas_call | solution.py:294
  77.0 0.8 %copy.13 = bf16[64,4096]{1,0:T(8,128)(2,1)} copy(bf16[64,4096]{1,0:T(8,128)(2,1)S(1)} %layer.1) | data formatting | bytes 1048576

commit v3 on v2

--- a/solution.py
+++ b/solution.py
@@ -53,6 +53,7 @@
     misc_sem, ksem, vsem, wsem, ssem, rsem, *parts,
 ):
     terms1, near1, line1, hs, terms2, near2, line2, ys = (parts[NG * i:NG * (i + 1)] for i in range(8))
+    far1, far2 = parts[8 * NG:]
     me = lax.axis_index("tp")
     barrier = pltpu.get_barrier_semaphore()
     for k in range(1, N):
@@ -188,6 +189,20 @@
     def gathered(buf, phase, g):
         arrived(buf[g].at[pl.ds(0, N - Q)], phase + 2, g)
 
+    def scatter_all(terms, far, phase, g):
+        for k in range(1, N):
+            to = lax.rem(me + k, N)
+            send(terms[g].at[to], far.at[k - 1], phase, g, to)
+
+    def gather_all(terms, far, buf, residual, phase, g):
+        arrived(far, phase, g)
+        total = terms[g][me].astype(F32)
+        for k in range(N - 1):
+            total = total + far[k].astype(F32)
+        buf[g][me] = (residual + total).astype(BF16)
+        for k in range(1, N):
+            send(buf[g].at[me], buf[g].at[me], phase + 2, g, lax.rem(me + k, N))
+
     def stage1(g):
         rows = seen[FIRST[g] // 8:(FIRST[g] + ROWS[g]) // 8].reshape(ROWS[g], QW)
         o = jnp.dot(rows.astype(BF16), wo[...], preferred_element_type=F32)
@@ -224,16 +239,26 @@
         o = jnp.dot(hidden, wd[...], preferred_element_type=F32)
         for j in range(N):
             terms2[g][j] = o[:, W * j:W * (j + 1)].astype(BF16)
-        scatter(terms2, near2, 3, g)
+        if g == NG - 1:
+            scatter_all(terms2, far2, 3, g)
+        else:
+            scatter(terms2, near2, 3, g)
 
     def stage5(g):
+        if g == NG - 1:
+            return gather_all(terms2, far2, ys, hs[g][me].astype(F32), 3, g)
         along(terms2, near2, line2, 3, g)
 
     def stage6(g):
+        if g == NG - 1:
+            return
         gather(line2, ys, lambda j: hs[g][mine * Q + j].astype(F32), 3, g)
 
     def stage7(g):
-        gathered(ys, 3, g)
+        if g == NG - 1:
+            arrived(ys[g].at[pl.ds(0, N - 1)], 5, g)
+        else:
+            gathered(ys, 3, g)
         for j in range(N):
             out[FIRST[g]:FIRST[g] + ROWS[g], W * j:W * (j + 1)] = ys[g][j]
 
@@ -304,7 +329,7 @@
             vmem((B // 8, 8, QW), F32), vmem((max(ROWS), D), BF16),
             dma((5,)), dma((NS,)), dma((NS,)), dma((4,)),
             dma((6, NG)), dma((6, NG)),
-        ] + [vmem((*n, r, W), BF16) for n in ((N,), (Q - 1, Q), (Z, Q), (N,)) * 2 for r in ROWS],
+        ] + [vmem((*n, r, W), BF16) for n in ((N,), (Q - 1, Q), (Z, Q), (N,)) * 2 for r in ROWS] + [vmem((N - 1, ROWS[-1], W), BF16)] * 2,
         compiler_params=pltpu.CompilerParams(collective_id=0, has_side_effects=True, vmem_limit_bytes=65994752),
         name="layer",
     )(x, k, v, gain_a.reshape(D // 128, 128), wq, wo, gain_m.reshape(D // 128, 128), w_gate, w_up, w_down, jnp.asarray(tables()))

time: 78 us -> 77.1 us (0.988)
  Pallas kernels: 77 us -> 76.1 us
    pallas_call x1, Pallas kernels: 77 us -> 76.1 us  [layer(): pl.pallas_call(kernel, out_shape=pltpu.VMEM((B, D), BF16), in_specs=[pl.B...]
where the time goes in v3:
time: 77.1 us; the launch traced here: 76.9 us
  Pallas kernels  76.1 us (99%)
  local copies, waits for them, and re-layouts  0.8 us (1%)
    pallas_call x1, Pallas kernels, layer(): pl.pallas_call(kernel, out_shape=pltpu.VMEM((B, D), BF16), in_specs=[pl.B...  76.1 us

profile of v3, /device:TPU:0, one launch (start us, length us, event | category | flops | bytes accessed | tf_op | source)
XLA Modules:
  0.0 76.9 jit_solution(10515340676671555115)
XLA Ops:
  0.0 76.1 %layer.1 = bf16[64,4096]{1,0:T(8,128)(2,1)S(1)} custom-call(bf16[64,4096]{1,0:T(8,128)(2,1)} %x_hbm.1, bf16[16384,2048]{1,0:T(8,128)(2,1)} %bitcast.1.k_hbm, bf16[16384,2048]{1,0:T(8,128)(2,1)} %bitcast.3.v_hbm, bf16[32,128]{1,0:T(8,128)(2,1)} %bitcast.8, bf16[4096,256]{1,0:T(8,128)(2,1)} %wq_hbm.1, bf16[256,4096]{1,0:T(8,128)(2,1)} %wo_hbm.1, ...), custom_call_target="tpu_custom_call" | custom-call | tf_op jit(solution)/shard_map/layer/pallas_call | solution.py:319
  76.1 0.8 %copy.13 = bf16[64,4096]{1,0:T(8,128)(2,1)} copy(bf16[64,4096]{1,0:T(8,128)(2,1)S(1)} %layer.1) | data formatting | bytes 1048576
